TPU v7x, 128 devices: a whole 4x4x4 slice. The times are simulated.
128 devices in a mesh: pool: 128 (over z, y, x, core).
Axes of the slice: x: 4, y: 4, z: 4, core: 2. Of those that a mesh axis runs over, the one named last changes fastest.
Arguments:
- queries: bfloat16 [128, 128, 64, 128], P('pool')
- k_new: bfloat16 [128, 128, 8, 128], P('pool')
- v_new: bfloat16 [128, 128, 8, 128], P('pool')
- k_pool: bfloat16 [4096, 16, 8, 128], P('pool')
- v_pool: bfloat16 [4096, 16, 8, 128], P('pool')
- block_table: int32 [128, 64], replicated
- write_ids: int32 [128, 8], P('pool')
Outputs:
- output 1: bfloat16 [128, 128, 64, 128], P('pool')
- output 2: bfloat16 [4096, 16, 8, 128], P('pool')
- output 3: bfloat16 [4096, 16, 8, 128], P('pool')
All inputs are finite; a program needn't handle non-finite values.
Results may differ from a plain program's by a relative error of at most 0.00941793.
Values are sent between devices in bfloat16 or wider.
A program may use at most 1 GiB of HBM per device.

v0:
```python
import jax
import jax.numpy as jnp
from jax import lax
from jax.experimental import pallas as pl
from jax.experimental.pallas import tpu as pltpu
from jax.sharding import PartitionSpec as P

MESH = pl.DeviceIdType.MESH
PLANES = 4
PLANE = 32
Z_CAP = 10
PAIR_CAP = 2
N_CH = 8
GROUP = 8
TILE = 64
LOG2E = 1.4426950408889634
RING = 4
GROUP_CAP = 10
LAG = 3
STEPS = (1, 3, 2)


def attend_head(q_ref, kv, new, out_ref, ch):
    chunk_len, head_dim = q_ref.shape[0], q_ref.shape[2]
    scale = head_dim ** -0.5 * LOG2E
    heads = pl.ds(ch * GROUP, GROUP)
    k_pref, v_pref = kv(0), kv(1)
    k_new, v_new = new(0), new(1)

    def nt(a, b):
        return lax.dot_general(a, b, (((1,), (1,)), ((), ())), preferred_element_type=jnp.float32)

    @pl.loop(0, chunk_len // TILE)
    def _(t):
        tokens = pl.ds(t * TILE, TILE)
        q = q_ref[tokens, heads, :].astype(jnp.float32).reshape(TILE * GROUP, head_dim).astype(jnp.bfloat16)
        s_pref = nt(q, k_pref)
        s_self = nt(q, k_new)
        token = t * TILE + lax.broadcasted_iota(jnp.int32, s_self.shape, 0) // GROUP
        s_self = jnp.where(token >= lax.broadcasted_iota(jnp.int32, s_self.shape, 1), s_self, -jnp.inf)
        top = jnp.maximum(jnp.max(s_pref, axis=1, keepdims=True), jnp.max(s_self, axis=1, keepdims=True))
        e_pref = jnp.exp2((s_pref - top) * scale)
        e_self = jnp.exp2((s_self - top) * scale)
        inv = 1.0 / (jnp.sum(e_pref, axis=1, keepdims=True) + jnp.sum(e_self, axis=1, keepdims=True))
        p_pref = (e_pref * inv).astype(jnp.bfloat16)
        p_self = (e_self * inv).astype(jnp.bfloat16)
        acc = jnp.dot(p_pref, v_pref, preferred_element_type=jnp.float32) + jnp.dot(p_self, v_new, preferred_element_type=jnp.float32)
        out_ref[tokens, heads, :] = acc.reshape(TILE, GROUP, head_dim).astype(jnp.bfloat16)


def head_major(src, wide, store, blocks):
    for i in range(blocks):
        tokens, heads, dim = wide.shape[1:]
        slot = i % wide.shape[0]
        wide[slot] = src(i).astype(jnp.float32)
        flat = wide.at[slot].reshape(tokens * heads, dim)
        for h in range(heads):
            store(i, h, flat[pl.ds(h, tokens, stride=heads), :].astype(jnp.bfloat16))


def prepare_kernel(wid_ref, table_ref, k_pool_hbm, v_pool_hbm, k_new_hbm, v_new_hbm, k_out_hbm, v_out_hbm, fits_ref, first_ref, second_ref, zsend_ref,
                   k_pool, v_pool, k_new, v_new, named, idx_vec, idx_smem, wide, in_sem, out_sem, idx_sem):
    me = lax.axis_index('pool')
    my_z, my_pos = me // PLANE, lax.rem(me, PLANE)
    per_dev = k_pool.shape[0]
    n_pref, n_row = table_ref.shape
    n_dev = n_row
    loads = [pltpu.make_async_copy(src, dst, in_sem.at[i]) for i, (src, dst) in enumerate(
        ((k_pool_hbm, k_pool), (v_pool_hbm, v_pool), (k_new_hbm, k_new), (v_new_hbm, v_new)))]
    for copy in loads:
        copy.start()

    def iota(shape, dim):
        return lax.broadcasted_iota(jnp.int32, shape, dim)

    def nt(x, y):
        return lax.dot_general(x, y, (((1,), (1,)), ((), ())), preferred_element_type=jnp.float32)

    def one_hot(row, rows):
        return jnp.where(iota((rows, n_row), 0) == row, 1.0, 0.0).astype(jnp.bfloat16)

    counts = jnp.zeros((n_dev, per_dev), jnp.float32)
    step = 8
    for e in range(0, n_pref, step):
        rows = [table_ref[e + i:e + i + 1, :] for i in range(step)]
        hot_owner = jnp.concatenate([one_hot(row // per_dev, n_dev) for row in rows], axis=1)
        hot_local = jnp.concatenate([one_hot(row % per_dev, per_dev) for row in rows], axis=1)
        counts = counts + nt(hot_owner, hot_local)
    is_named = jnp.where(counts > 0, 1.0, 0.0)
    named[...] = is_named
    most_named = jnp.max(jnp.sum(is_named, axis=1, keepdims=True), axis=0, keepdims=True)

    table = table_ref[...]
    owner, local = table // per_dev, table % per_dev
    col, plane = owner % PLANE, owner // PLANE
    most_in_col = jnp.zeros((1, n_row), jnp.int32)
    for c in range(PLANE):
        most_in_col = jnp.maximum(most_in_col, jnp.sum(jnp.where(col == c, 1, 0), axis=0, keepdims=True))
    most_in_col = jnp.max(most_in_col, axis=1, keepdims=True)

    key = plane * per_dev + local
    n_key = PLANES * per_dev

    def ends(q):
        match = col == q
        return (jnp.min(jnp.where(match, key, n_key - 1), axis=0, keepdims=True), jnp.max(jnp.where(match, key, 0), axis=0, keepdims=True))

    def flag(mask):
        return jnp.where(mask, 1.0, 0.0).astype(jnp.bfloat16)

    def members(n_group, plane_of, index_of):
        group, row = iota((n_group, n_row), 0), iota((n_group, n_row), 1)
        at = jnp.where(group // RING % 2 == 0, row // 8 % RING, row // 2 % RING)
        return flag((row // PLANE == plane_of(group)) & (at == index_of(group)))

    all_groups = members(2 * RING * PLANES, lambda g: g // (2 * RING), lambda g: g % RING)

    def widest(q, most):
        first, last = ends(q)
        named_by = nt(all_groups, flag((iota((n_key, n_row), 0) == first) | (iota((n_key, n_row), 0) == last)))
        return jnp.maximum(most, jnp.sum(jnp.where(named_by > 0, 1.0, 0.0), axis=1, keepdims=True))

    most_in_group = lax.fori_loop(0, PLANE, widest, jnp.zeros((2 * RING * PLANES, 1), jnp.float32), unroll=4)
    most_in_group = jnp.max(most_in_group, axis=0, keepdims=True)
    fits = jnp.where((most_named <= Z_CAP) & (most_in_col <= PAIR_CAP) & (most_in_group <= GROUP_CAP), 1, 0)
    fits_ref[...] = jnp.broadcast_to(fits, fits_ref.shape)

    mine = jnp.concatenate([named[pl.ds(z * PLANE + my_pos, 1), :] for z in range(PLANES)], axis=0)
    before = jnp.where(iota((per_dev, per_dev), 0) < iota((per_dev, per_dev), 1), 1.0, 0.0).astype(jnp.bfloat16)
    rank = jnp.dot(mine.astype(jnp.bfloat16), before, preferred_element_type=jnp.float32)
    own = iota(rank.shape, 0) == my_z
    own_rank = jnp.sum(jnp.where(own & (mine > 0), rank, 0.0) + jnp.where(own & (mine == 0), 1000.0, 0.0), axis=0, keepdims=True)
    hit = iota((16, per_dev), 0).astype(jnp.float32) == own_rank
    chosen = jnp.sum(jnp.where(hit, iota((16, per_dev), 1), 0), axis=1, keepdims=True)
    idx_vec[...] = jnp.broadcast_to(chosen, idx_vec.shape)
    to_smem = pltpu.make_async_copy(idx_vec, idx_smem, idx_sem)
    to_smem.start()

    slot = jnp.minimum(rank, Z_CAP - 1.0) + (iota(rank.shape, 0) * Z_CAP).astype(jnp.float32)
    slot_row = jnp.zeros((1, n_key), jnp.float32)
    for z in range(PLANES):
        place = flag(iota((per_dev, n_key), 1) == iota((per_dev, n_key), 0) + z * per_dev)
        slot_row = slot_row + jnp.dot(slot[z:z + 1].astype(jnp.bfloat16), place, preferred_element_type=jnp.float32)
    groups = members(2 * RING, lambda g: my_z, lambda g: g % RING)
    before_key = flag(iota((n_key, n_key), 0) < iota((n_key, n_key), 1))
    my_y, my_x, my_c = my_pos // 8, lax.rem(my_pos // 2, RING), lax.rem(my_pos, 2)

    def lists(q):
        hots = [flag(iota((n_key, n_row), 0) == end) for end in ends(q)]
        listed = jnp.where(nt(groups, hots[0]) + nt(groups, hots[1]) > 0, 1.0, 0.0)
        return hots, listed, jnp.dot(listed.astype(jnp.bfloat16), before_key, preferred_element_type=jnp.float32)

    _, listed, place = lists(my_pos)
    first_step = jnp.zeros((2 * RING, 128), jnp.int32)
    for i in range(GROUP_CAP):
        at = jnp.sum(jnp.where((listed > 0) & (place == i), slot_row, 0.0), axis=1, keepdims=True).astype(jnp.int32)
        first_step = jnp.where(iota(first_step.shape, 1) == i, at, first_step)
    first_ref[...] = first_step
    for part in range(2):
        for src in range(RING):
            q = (src * 8 + my_x * 2 + my_c) if part == 0 else (my_y * 8 + src * 2 + my_c)
            mine_at = my_y if part == 0 else RING + my_x
            hots, listed, place = lists(q)
            for end in range(PAIR_CAP):
                found = jnp.dot(place.astype(jnp.bfloat16), hots[end], preferred_element_type=jnp.float32)
                found = jnp.sum(jnp.where(iota(found.shape, 0) == mine_at, found, 0.0), axis=0, keepdims=True)
                line = (part * RING + src) * PAIR_CAP + end
                second_ref[line:line + 1, :] = jnp.minimum(found.astype(jnp.int32), GROUP_CAP - 1) + src * GROUP_CAP

    for copy in loads:
        copy.wait()
    pools = [pltpu.make_async_copy(src, dst, out_sem.at[i]) for i, (src, dst) in enumerate(((k_pool, k_out_hbm), (v_pool, v_out_hbm)))]
    for copy in pools:
        copy.start()
    to_smem.wait()
    for part, pool in enumerate((k_pool, v_pool)):
        def store(i, h, x):
            zsend_ref[h, i, part] = x
        head_major(lambda i: pool[idx_smem[i, 0]], wide, store, Z_CAP)
    for copy in pools:
        copy.wait()
    writes = []
    for i in range(k_new.shape[0]):
        for part, (src, dst) in enumerate(((k_new, k_out_hbm), (v_new, v_out_hbm))):
            writes.append(pltpu.make_async_copy(src.at[i], dst.at[wid_ref[0, i]], in_sem.at[2 * i + part]))
            writes[-1].start()
    for copy in writes:
        copy.wait()


def prepare(write_ids, table_t, k_pool, v_pool, k_new, v_new):
    per_dev, tokens, heads, dim = k_pool.shape
    n_row = table_t.shape[1]
    new_blocks = k_new.shape[0]
    vmem, smem, hbm = (pl.BlockSpec(memory_space=m) for m in (pltpu.VMEM, pltpu.SMEM, pl.ANY))
    return pl.pallas_call(
        prepare_kernel,
        out_shape=[jax.ShapeDtypeStruct(k_pool.shape, k_pool.dtype), jax.ShapeDtypeStruct(v_pool.shape, v_pool.dtype),
                   jax.ShapeDtypeStruct((8, 128), jnp.int32), jax.ShapeDtypeStruct((2 * RING, 128), jnp.int32),
                   jax.ShapeDtypeStruct((2 * RING * PAIR_CAP, n_row), jnp.int32),
                   jax.ShapeDtypeStruct((N_CH, Z_CAP, 2, tokens, dim), k_pool.dtype)],
        in_specs=[smem, vmem, hbm, hbm, hbm, hbm],
        out_specs=[hbm, hbm, vmem, vmem, vmem, vmem],
        scratch_shapes=[pltpu.VMEM(k_pool.shape, k_pool.dtype), pltpu.VMEM(k_pool.shape, k_pool.dtype),
                        pltpu.VMEM(k_new.shape, k_pool.dtype), pltpu.VMEM(k_new.shape, k_pool.dtype),
                        pltpu.VMEM((n_row, per_dev), jnp.float32), pltpu.VMEM((16, 128), jnp.int32), pltpu.SMEM((16, 128), jnp.int32),
                        pltpu.VMEM((4, tokens, heads, dim), jnp.float32),
                        pltpu.SemaphoreType.DMA((2 * new_blocks,)), pltpu.SemaphoreType.DMA((2,)), pltpu.SemaphoreType.DMA],
        compiler_params=pltpu.CompilerParams(vmem_limit_bytes=32 << 20),
        name='prepare',
    )(write_ids, table_t, k_pool, v_pool, k_new, v_new)


def exchange_kernel(first_ref, second_ref, q_hbm, zsend_hbm, k_new_hbm, v_new_hbm, out_hbm, q_ref, out_ref, recv_k, recv_v, k_new, v_new,
                    new_t, wide, zsend, *scratch):
    zrecv, send1, recv1, send2 = (scratch[:N_CH], scratch[N_CH:3 * N_CH], scratch[3 * N_CH:5 * N_CH], scratch[5 * N_CH:7 * N_CH])
    zs_sem, zr_sem, s1_sem, r1_sem, s2_sem, r2_sem, in_sem, out_sem = scratch[7 * N_CH:]
    me = lax.axis_index('pool')
    my_z, my_pos = me // PLANE, lax.rem(me, PLANE)
    base = my_z * PLANE
    y, x, c = my_pos // 8, lax.rem(my_pos // 2, RING), lax.rem(my_pos, 2)
    head_dim = q_ref.shape[2]

    def z_peer(d):
        return lax.rem(my_z + d, PLANES) * PLANE + my_pos

    def y_peer(d, dc):
        return base + lax.rem(y + d, RING) * 8 + x * 2 + lax.rem(c + dc, 2)

    def x_peer(d, dc):
        return base + y * 8 + lax.rem(x + d, RING) * 2 + lax.rem(c + dc, 2)

    barrier = pltpu.get_barrier_semaphore()
    peers = [z_peer(d) for d in STEPS] + [peer(d, dc) for d in STEPS for dc in range(2) for peer in (y_peer, x_peer)] + [y_peer(0, 1)]
    for peer in peers:
        pl.semaphore_signal(barrier, inc=1, device_id=(peer,), device_id_type=MESH)

    loads = [pltpu.make_async_copy(src, dst, in_sem.at[i]) for i, (src, dst) in enumerate(
        ((zsend_hbm, zsend), (k_new_hbm, k_new), (v_new_hbm, v_new), (q_hbm, q_ref)))]
    for copy in loads:
        copy.start()

    def remote(src, dst, send_sem, recv_sem, peer):
        return pltpu.make_async_remote_copy(
            src_ref=src, dst_ref=dst, send_sem=send_sem, recv_sem=recv_sem, device_id=(peer,), device_id_type=MESH)

    def wait_bytes(ref, sem):
        pltpu.make_async_copy(ref, ref, sem).wait()

    def z_wait(ch, sem):
        wait_bytes(zrecv[ch].at[pl.ds(0, (PLANES - 1) * Z_CAP)], sem.at[ch])

    def wait1(i, sem):
        wait_bytes(recv1[i].at[pl.ds(0, (RING - 1) * GROUP_CAP)], sem.at[i])

    def wait2(i, sem):
        wait_bytes(send2[i].at[pl.ds(0, 2 * RING - 1)], sem.at[i])

    def step1(ch):
        for part in range(2):
            i = 2 * ch + part
            for g in range(RING):
                for s in range(GROUP_CAP):
                    send1[i][g, s] = zrecv[ch][first_ref[part * RING + g, s], part]
            mine = y if part == 0 else x
            recv1[i][pl.ds(mine * GROUP_CAP, GROUP_CAP)] = send1[i][mine]
        for d in STEPS:
            for part in range(2):
                i = 2 * ch + part
                mine, peer = (y, y_peer(d, 0)) if part == 0 else (x, x_peer(d, 0))
                remote(send1[i].at[lax.rem(mine + d, RING)], recv1[i].at[pl.ds(mine * GROUP_CAP, GROUP_CAP)],
                       s1_sem.at[i], r1_sem.at[i], peer).start()

    def step2(ch):
        for part in range(2):
            i = 2 * ch + part
            wait1(i, r1_sem)

            @pl.loop(0, RING)
            def _(to):
                for core in range(2):
                    row = base + ((y * 8 + to * 2) if part == 0 else (to * 8 + x * 2)) + core
                    for src in range(RING):
                        for end in range(PAIR_CAP):
                            send2[i][to * 2 + core, src, end * 16:(end + 1) * 16, :] = recv1[i][second_ref[(part * RING + src) * PAIR_CAP + end, row]]

        recv_k[ch, :, x, c] = send2[2 * ch][x * 2 + c]
        recv_v[ch, y, :, c] = send2[2 * ch + 1][y * 2 + c]
        for d in STEPS + (0,):
            for dc in range(2):
                for part in range(2):
                    if (d, dc) == (0, 0):
                        continue
                    i = 2 * ch + part
                    mine, peer = (x, x_peer(d, dc)) if part == 0 else (y, y_peer(d, dc))
                    dst = recv_k.at[ch, :, x, c] if part == 0 else recv_v.at[ch, y, :, c]
                    remote(send2[i].at[lax.rem(mine + d, RING) * 2 + lax.rem(c + dc, 2)], dst, s2_sem.at[i], r2_sem.at[i], peer).start()

    def out_copy(ch):
        heads = pl.ds(ch * GROUP, GROUP)
        return pltpu.make_async_copy(out_ref.at[:, heads, :], out_hbm.at[:, heads, :], out_sem.at[ch])

    def attend(ch):
        wait2(2 * ch, r2_sem)
        wait2(2 * ch + 1, r2_sem)
        recv = (recv_k, recv_v)
        attend_head(q_ref, lambda part: recv[part][ch].reshape(-1, head_dim), lambda part: new_t[ch, part], out_ref, ch)
        out_copy(ch).start()

    loads[0].wait()
    pl.semaphore_wait(barrier, len(peers))
    for ch in range(N_CH):
        for d in STEPS:
            remote(zsend.at[ch], zrecv[ch].at[pl.ds(my_z * Z_CAP, Z_CAP)], zs_sem.at[ch], zr_sem.at[ch], z_peer(d)).start()
    for ch in range(N_CH):
        zrecv[ch][pl.ds(my_z * Z_CAP, Z_CAP)] = zsend[ch]
    for part, block in enumerate((k_new, v_new)):
        loads[1 + part].wait()

        def store(i, h, x):
            new_t[h, part, i * 16:(i + 1) * 16, :] = x
        head_major(lambda i: block[i], wide, store, block.shape[0])
    loads[3].wait()
    for t in range(N_CH + LAG):
        if t < N_CH:
            z_wait(t, zr_sem)
            step1(t)
        if 1 <= t <= N_CH:
            step2(t - 1)
        if t >= LAG:
            attend(t - LAG)
    for ch in range(N_CH):
        z_wait(ch, zs_sem)
        out_copy(ch).wait()
    for i in range(2 * N_CH):
        wait1(i, s1_sem)
        wait2(i, s2_sem)


def exchange_attention(first, second, q, zsend, k_new, v_new):
    tokens, dim = zsend.shape[3:]
    dtype = q.dtype
    hbm, smem = pl.BlockSpec(memory_space=pl.ANY), pl.BlockSpec(memory_space=pltpu.SMEM)
    recv = pltpu.VMEM((N_CH, RING, RING, 2, PAIR_CAP * tokens, dim), dtype)
    return pl.pallas_call(
        exchange_kernel,
        out_shape=jax.ShapeDtypeStruct(q.shape, dtype),
        in_specs=[smem, smem, hbm, hbm, hbm, hbm],
        out_specs=hbm,
        scratch_shapes=[pltpu.VMEM(q.shape, dtype), pltpu.VMEM(q.shape, dtype), recv, recv,
                        pltpu.VMEM(k_new.shape, dtype), pltpu.VMEM(v_new.shape, dtype), pltpu.VMEM((N_CH, 2, q.shape[0], q.shape[2]), dtype),
                        pltpu.VMEM((4,) + k_new.shape[1:], jnp.float32), pltpu.VMEM(zsend.shape, dtype)]
        + [pltpu.VMEM((PLANES * Z_CAP, 2, tokens, dim), dtype)] * N_CH
        + [pltpu.VMEM((RING, GROUP_CAP, tokens, dim), dtype)] * (2 * N_CH)
        + [pltpu.VMEM((RING * GROUP_CAP, tokens, dim), dtype)] * (2 * N_CH)
        + [pltpu.VMEM((2 * RING, RING, PAIR_CAP * tokens, dim), dtype)] * (2 * N_CH)
        + [pltpu.SemaphoreType.DMA((N_CH,))] * 2 + [pltpu.SemaphoreType.DMA((2 * N_CH,))] * 4 + [pltpu.SemaphoreType.DMA((N_CH,))] * 2,
        compiler_params=pltpu.CompilerParams(collective_id=0, has_side_effects=True, vmem_limit_bytes=56 << 20),
        name='exchange_attention',
    )(first, second, q, zsend, k_new, v_new)


def attention_kernel(q_ref, kv_ref, new_ref, out_ref):
    head_dim = q_ref.shape[2]
    attend_head(q_ref, lambda part: kv_ref[0, :, part].reshape(-1, head_dim), lambda part: new_ref[0, part], out_ref, 0)


def attention(q, kv, new):
    chunk_len, q_heads, head_dim = q.shape
    return pl.pallas_call(
        attention_kernel,
        grid=(N_CH,),
        out_shape=jax.ShapeDtypeStruct(q.shape, q.dtype),
        in_specs=[pl.BlockSpec((chunk_len, GROUP, head_dim), lambda c: (0, c, 0)),
                  pl.BlockSpec((1,) + kv.shape[1:], lambda c: (c, 0, 0, 0, 0)),
                  pl.BlockSpec((1,) + new.shape[1:], lambda c: (c, 0, 0, 0))],
        out_specs=pl.BlockSpec((chunk_len, GROUP, head_dim), lambda c: (0, c, 0)),
        compiler_params=pltpu.CompilerParams(vmem_limit_bytes=48 << 20),
        name='attention',
    )(q, kv, new)


def by_chunk(k, v):
    n, t, h, d = k.shape
    both = jnp.stack([k, v], axis=1).reshape(n, 2, t, N_CH, h // N_CH, d)
    return both.transpose(0, 3, 1, 4, 2, 5).reshape(n, N_CH, 2 * h // N_CH, t, d)


def solution(mesh):
    n_dev = mesh.shape['pool']

    def padded_exchange(k_pool, v_pool, block_table):
        per_dev = k_pool.shape[0]
        n_pref = block_table.shape[1]
        my_index = lax.axis_index('pool')
        pair_cap = 2
        owners = block_table // per_dev
        owned_here = (owners == my_index).astype(jnp.int32)
        send_slot = jnp.where(owned_here > 0, jnp.cumsum(owned_here, axis=1) - 1, pair_cap)
        dest_dev = jnp.broadcast_to(jnp.arange(n_dev)[:, None], send_slot.shape)
        send_ids = jnp.zeros((n_dev, pair_cap), jnp.int32).at[dest_dev, send_slot].set(block_table % per_dev, mode='drop')
        k_recv = lax.all_to_all(k_pool[send_ids], 'pool', 0, 0, tiled=True)
        v_recv = lax.all_to_all(v_pool[send_ids], 'pool', 0, 0, tiled=True)
        my_owners = lax.dynamic_slice_in_dim(owners, my_index, 1, 0).reshape(-1)
        from_owner = (my_owners[:, None] == jnp.arange(n_dev)[None, :]).astype(jnp.int32)
        slot_rank = jnp.sum(from_owner * (jnp.cumsum(from_owner, axis=0) - 1), axis=1)
        recv_idx = my_owners * pair_cap + slot_rank
        flat = (n_dev * pair_cap,) + k_pool.shape[1:]
        pairs = by_chunk(k_recv.reshape(flat)[recv_idx], v_recv.reshape(flat)[recv_idx])
        parts, t, d = pairs.shape[2:]
        pairs = pairs.reshape(n_pref // PAIR_CAP, PAIR_CAP, N_CH, parts, t, d).transpose(2, 0, 3, 1, 4, 5)
        return pairs.reshape(N_CH, n_pref // PAIR_CAP, parts, PAIR_CAP * t, d)

    def local_step(queries, k_new, v_new, k_pool, v_pool, block_table, write_ids):
        block_len = k_pool.shape[1]
        new_shape = (queries.shape[1] // block_len, block_len) + k_new.shape[2:]
        k_blocks, v_blocks = k_new.reshape(new_shape), v_new.reshape(new_shape)
        k_pool_out, v_pool_out, fits, first, second, zsend = prepare(write_ids, block_table.T, k_pool, v_pool, k_blocks, v_blocks)
        attn_out = lax.cond(
            fits[0, 0] > 0,
            lambda: exchange_attention(first, second, queries[0], zsend, k_blocks, v_blocks),
            lambda: attention(queries[0], padded_exchange(k_pool, v_pool, block_table), by_chunk(k_new, v_new)[0]))[None]
        return attn_out, k_pool_out, v_pool_out

    row_spec = P('pool')
    return jax.shard_map(local_step, mesh=mesh, in_specs=(row_spec, row_spec, row_spec, row_spec, row_spec, P(), row_spec), out_specs=(row_spec, row_spec, row_spec), check_vma=False)
```

profile of v0, /device:TPU:1, one launch (start us, length us, event | category | flops | bytes accessed | tf_op | source)
XLA Modules:
  0.0 75.4 jit_solution(3509004432772324070)
XLA Ops:
  0.6 0.0 copy-start
  0.6 0.6 copy-done
  1.3 10.3 %prepare.1 = (bf16[32,16,8,128]{3,2,1,0:T(8,128)(2,1)}, bf16[32,16,8,128]{3,2,1,0:T(8,128)(2,1)}, s32[8,128]{1,0:T(8,128)S(1)}, s32[8,128]{1,0:T(8,128)S(1)}, s3...) custom-call(s32[1,8]{1,0:T(1,128)S(1)} %copy-done, s32[64,128]{1,0:T(8,128)} %bitcast.60, ...), custom_call_target="tpu_custom_call" | custom-call | tf_op jit(solution)/shard_map/prepare/pallas_call | solution.py:196
  11.6 0.5 slice.3
  12.8 61.3 %conditional.1 = (bf16[1,128,64,128]{3,2,1,0:T(8,128)(2,1)S(1)}) conditional(s32[]{:T(128)} %bitcast.34, (bf16[1,128,64,128]{3,2,1,0:T(8,128)(2,1)}, s32[128,64]{0,1:T(8,128)}, bf16[32,16,8,128]{3,2,1,0:T(8,128)(2,1)}, bf16[32,16,8,128]{3,2,1,0:T(8,128)(2,1)}, bf16[1,128,8,128]{3,2,1,0:T(8,128)(2,1)}, ...), branch_computations={%region_0.5_spmd, %region_5.6_spmd} | conditional | flops 3845125 | bytes 131044656 | solution.py:419
  13.0 60.7 %exchange_attention.1 = bf16[128,64,128]{2,1,0:T(8,128)(2,1)S(1)} custom-call(s32[8,128]{1,0:T(8,128)S(1)} %get-tuple-element.34.first_ref, s32[16,128]{1,0:T(8,128)S(1)} %get-tuple-element.35.second_ref, bf16[128,64,128]{2,1,0:T(8,128)(2,1)} %bitcast.51, bf16[8,10,2,16,128]{4,3,2,1,0:T(8,128)(2,1)} %get-tuple-element.37.zsend_hbm, ...), custom_call_target="tpu_custom_call" | custom-call | tf_op jit(solution)/shard_map/cond/branch_1_fun/exchange_attention/pallas_call | solution.py:345
  74.1 1.3 %copy.30 = bf16[1,128,64,128]{3,2,1,0:T(8,128)(2,1)} copy(bf16[1,128,64,128]{3,2,1,0:T(8,128)(2,1)S(1)} %get-tuple-element.85) | data formatting | bytes 4194304
Async XLA Ops:
  0.6 0.7 copy-start
where the time goes:
time: 75.9 us; the launch traced here: 75.4 us
  Pallas kernels  71.1 us (94%)
  local copies, waits for them, and re-layouts  2.48 us (3%)
  between operations  1.31 us (2%)
    pallas_call x1, Pallas kernels, exchange_attention(): pl.pallas_call(exchange_kernel, out_shape=jax.ShapeDtypeStruct(q.shape, d...  60.7 us
    pallas_call x1, Pallas kernels, prepare(): pl.pallas_call(prepare_kernel, out_shape=[jax.ShapeDtypeStruct(k_pool.sha...  10.3 us
    unnamed x3, local copies, waits for them, and re-layouts  1.97 us

commit v1 on v0

v1 whole, which is shorter than its diff:
```python
import functools

import jax
import jax.numpy as jnp
from jax import lax
from jax.experimental import pallas as pl
from jax.experimental.pallas import tpu as pltpu
from jax.sharding import PartitionSpec as P

MESH = pl.DeviceIdType.MESH
PLANES = 4
PLANE = 32
Z_CAP = 10
PAIR_CAP = 2
N_CH = 8
GROUP = 8
TILE = 32
LOG2E = 1.4426950408889634
RING = 4
GROUP_CAP = 10
LAG = 3
STEPS = (1, 3, 2)


def attend_head(q_ref, kv, new, out_ref, ch):
    chunk_len, head_dim = q_ref.shape[0], q_ref.shape[2]
    scale = head_dim ** -0.5 * LOG2E
    heads = pl.ds(ch * GROUP, GROUP)
    k_pref, v_pref = kv(0), kv(1)
    k_new, v_new = new(0), new(1)

    def scores(t):
        q = q_ref[pl.ds(t * TILE, TILE), heads, :].astype(jnp.float32).reshape(TILE * GROUP, head_dim).astype(jnp.bfloat16)
        return nt(q, k_pref), nt(q, k_new)

    n_tile = chunk_len // TILE
    ahead = scores(0)
    for t in range(n_tile):
        s_pref, s_self = ahead
        if t + 1 < n_tile:
            ahead = scores(t + 1)
        token = t * TILE + lax.broadcasted_iota(jnp.int32, s_self.shape, 0) // GROUP
        s_self = jnp.where(token >= lax.broadcasted_iota(jnp.int32, s_self.shape, 1), s_self, -jnp.inf)
        top = jnp.maximum(jnp.max(s_pref, axis=1, keepdims=True), jnp.max(s_self, axis=1, keepdims=True))
        e_pref = jnp.exp2((s_pref - top) * scale)
        e_self = jnp.exp2((s_self - top) * scale)
        inv = 1.0 / (jnp.sum(e_pref, axis=1, keepdims=True) + jnp.sum(e_self, axis=1, keepdims=True))
        p_pref = (e_pref * inv).astype(jnp.bfloat16)
        p_self = (e_self * inv).astype(jnp.bfloat16)
        acc = jnp.dot(p_pref, v_pref, preferred_element_type=jnp.float32) + jnp.dot(p_self, v_new, preferred_element_type=jnp.float32)
        out_ref[pl.ds(t * TILE, TILE), heads, :] = acc.reshape(TILE, GROUP, head_dim).astype(jnp.bfloat16)


def head_major(src, wide, store, blocks):
    for i in range(blocks):
        tokens, heads, dim = wide.shape[1:]
        slot = i % wide.shape[0]
        wide[slot] = src(i).astype(jnp.float32)
        flat = wide.at[slot].reshape(tokens * heads, dim)
        for h in range(heads):
            store(i, h, flat[pl.ds(h, tokens, stride=heads), :].astype(jnp.bfloat16))


def iota(shape, dim):
    return lax.broadcasted_iota(jnp.int32, shape, dim)


def flag(mask):
    return jnp.where(mask, 1.0, 0.0).astype(jnp.bfloat16)


def nt(a, b):
    return lax.dot_general(a, b, (((1,), (1,)), ((), ())), preferred_element_type=jnp.float32)


class Table:
    def __init__(self, table, per_dev):
        owner = table // per_dev
        self.per_dev, self.n_key, self.n_row = per_dev, PLANES * per_dev, table.shape[1]
        self.col = owner % PLANE
        self.key = owner // PLANE * per_dev + table % per_dev

    def hots(self, q):
        match = self.col == q
        ends = (jnp.min(jnp.where(match, self.key, self.n_key - 1), axis=0, keepdims=True), jnp.max(jnp.where(match, self.key, 0), axis=0, keepdims=True))
        return [flag(iota((self.n_key, self.n_row), 0) == end) for end in ends]

    def slots(self, q):
        first, last = self.hots(q)
        every = flag(iota((8, self.n_row), 0) >= 0)
        named = jnp.where(nt(every, first) + nt(every, last) > 0, 1.0, 0.0)
        i, j = iota((self.n_key, self.n_key), 0), iota((self.n_key, self.n_key), 1)
        before = flag((i < j) & (i // self.per_dev == j // self.per_dev))
        rank = jnp.dot(named.astype(jnp.bfloat16), before, preferred_element_type=jnp.float32)
        return named[:1], rank[:1]


def prepare_kernel(wid_ref, table_hbm, k_pool_hbm, v_pool_hbm, k_new_hbm, v_new_hbm, k_out_hbm, v_out_hbm, zsend_ref,
                   table_ref, k_pool, v_pool, k_new, v_new, idx_vec, idx_smem, wide, in_sem, out_sem, idx_sem):
    me = lax.axis_index('pool')
    my_z, my_pos = me // PLANE, lax.rem(me, PLANE)
    per_dev = k_pool.shape[0]
    get_table = pltpu.make_async_copy(table_hbm, table_ref, idx_sem)
    get_table.start()
    loads = [pltpu.make_async_copy(src, dst, in_sem.at[i]) for i, (src, dst) in enumerate(
        ((k_pool_hbm, k_pool), (v_pool_hbm, v_pool), (k_new_hbm, k_new), (v_new_hbm, v_new)))]
    for copy in loads:
        copy.start()
    get_table.wait()
    table = Table(table_ref[...], per_dev)
    named, rank = table.slots(my_pos)
    key = iota((16, table.n_key), 1)
    hit = (named > 0) & (rank == iota((16, table.n_key), 0).astype(jnp.float32)) & (key // per_dev == my_z)
    chosen = jnp.sum(jnp.where(hit, key % per_dev, 0), axis=1, keepdims=True)
    idx_vec[...] = jnp.broadcast_to(chosen, idx_vec.shape)
    to_smem = pltpu.make_async_copy(idx_vec, idx_smem, idx_sem)
    to_smem.start()

    for copy in loads:
        copy.wait()
    pools = [pltpu.make_async_copy(src, dst, out_sem.at[i]) for i, (src, dst) in enumerate(((k_pool, k_out_hbm), (v_pool, v_out_hbm)))]
    for copy in pools:
        copy.start()
    to_smem.wait()

    def send_blocks(part, pool):
        def store(i, h, x):
            zsend_ref[h, i, part] = x
        head_major(lambda i: pool[idx_smem[i, 0]], wide, store, Z_CAP)

    send_blocks(0, k_pool)
    for copy in pools:
        copy.wait()
    writes = []
    for i in range(k_new.shape[0]):
        for part, (src, dst) in enumerate(((k_new, k_out_hbm), (v_new, v_out_hbm))):
            writes.append(pltpu.make_async_copy(src.at[i], dst.at[wid_ref[0, i]], in_sem.at[2 * i + part]))
            writes[-1].start()
    send_blocks(1, v_pool)
    for copy in writes:
        copy.wait()


def prepare(write_ids, table_t, k_pool, v_pool, k_new, v_new):
    tokens, heads, dim = k_pool.shape[1:]
    vmem, smem, hbm = (pl.BlockSpec(memory_space=m) for m in (pltpu.VMEM, pltpu.SMEM, pl.ANY))
    return pl.pallas_call(
        prepare_kernel,
        out_shape=[jax.ShapeDtypeStruct(k_pool.shape, k_pool.dtype), jax.ShapeDtypeStruct(v_pool.shape, v_pool.dtype),
                   jax.ShapeDtypeStruct((N_CH, Z_CAP, 2, tokens, dim), k_pool.dtype)],
        in_specs=[smem, hbm, hbm, hbm, hbm, hbm],
        out_specs=[hbm, hbm, vmem],
        scratch_shapes=[pltpu.VMEM(table_t.shape, jnp.int32), pltpu.VMEM(k_pool.shape, k_pool.dtype), pltpu.VMEM(k_pool.shape, k_pool.dtype),
                        pltpu.VMEM(k_new.shape, k_pool.dtype), pltpu.VMEM(k_new.shape, k_pool.dtype),
                        pltpu.VMEM((16, 128), jnp.int32), pltpu.SMEM((16, 128), jnp.int32), pltpu.VMEM((4, tokens, heads, dim), jnp.float32),
                        pltpu.SemaphoreType.DMA((2 * k_new.shape[0],)), pltpu.SemaphoreType.DMA((2,)), pltpu.SemaphoreType.DMA],
        compiler_params=pltpu.CompilerParams(vmem_limit_bytes=32 << 20),
        name='prepare',
    )(write_ids, table_t, k_pool, v_pool, k_new, v_new)


def members(n_group, n_row, plane_of):
    group, row = iota((n_group, n_row), 0), iota((n_group, n_row), 1)
    at = jnp.where(group // RING % 2 == 0, row // 8 % RING, row // 2 % RING)
    return flag((row // PLANE == plane_of(group)) & (at == group % RING))


def capacity_check(table, named_by_column):
    groups = members(2 * RING * PLANES, table.n_row, lambda g: g // (2 * RING))
    n_group = groups.shape[0]

    def widest(q, most):
        first, last = table.hots(q)
        named = jnp.where(nt(groups, first) + nt(groups, last) > 0, 1.0, 0.0)
        named_by_column[pl.ds(q, 1), :] = jnp.max(named, axis=0, keepdims=True)
        return jnp.maximum(most, jnp.sum(named, axis=1, keepdims=True))

    most_in_group = lax.fori_loop(0, PLANE, widest, jnp.zeros((n_group, 1), jnp.float32), unroll=4)
    per_plane = flag(iota((table.n_key, 128), 0) // table.per_dev == iota((table.n_key, 128), 1))
    by_device = jnp.dot(named_by_column[...].astype(jnp.bfloat16), per_plane, preferred_element_type=jnp.float32)
    in_col = jnp.zeros((1, table.n_row), jnp.int32)
    for q in range(PLANE):
        in_col = jnp.maximum(in_col, jnp.sum(jnp.where(table.col == q, 1, 0), axis=0, keepdims=True))

    def top(a):
        return jnp.max(jnp.max(a, axis=1, keepdims=True), axis=0, keepdims=True)

    return jnp.where((top(in_col) <= PAIR_CAP) & (top(by_device) <= Z_CAP) & (top(most_in_group) <= GROUP_CAP), 1, 0)


def routing(table, my_z, my_y, my_x, my_c, first_ref, second_ref):
    n_key, n_row = table.n_key, table.n_row
    my_pos = my_y * 8 + my_x * 2 + my_c
    _, rank = table.slots(my_pos)
    slot_row = jnp.minimum(rank, Z_CAP - 1.0) + (iota(rank.shape, 1) // table.per_dev * Z_CAP).astype(jnp.float32)
    groups = members(2 * RING, n_row, lambda g: my_z)
    before = flag(iota((n_key, n_key), 0) < iota((n_key, n_key), 1))

    def lists(q):
        hots = table.hots(q)
        listed = jnp.where(nt(groups, hots[0]) + nt(groups, hots[1]) > 0, 1.0, 0.0)
        return hots, listed, jnp.dot(listed.astype(jnp.bfloat16), before, preferred_element_type=jnp.float32)

    _, listed, place = lists(my_pos)
    first_step = jnp.zeros((2 * RING, 128), jnp.int32)
    for i in range(GROUP_CAP):
        at = jnp.sum(jnp.where((listed > 0) & (place == i), slot_row, 0.0), axis=1, keepdims=True).astype(jnp.int32)
        first_step = jnp.where(iota(first_step.shape, 1) == i, at, first_step)
    first_ref[...] = jnp.clip(first_step, 0, PLANES * Z_CAP - 1)
    for part in range(2):
        for src in range(RING):
            q = (src * 8 + my_x * 2 + my_c) if part == 0 else (my_y * 8 + src * 2 + my_c)
            mine_at = my_y if part == 0 else RING + my_x
            hots, _, place = lists(q)
            for end in range(PAIR_CAP):
                found = jnp.dot(place.astype(jnp.bfloat16), hots[end], preferred_element_type=jnp.float32)
                found = jnp.sum(jnp.where(iota(found.shape, 0) == mine_at, found, 0.0), axis=0, keepdims=True)
                line = (part * RING + src) * PAIR_CAP + end
                second_ref[line:line + 1, :] = jnp.clip(found.astype(jnp.int32), 0, GROUP_CAP - 1) + src * GROUP_CAP


def exchange_kernel(per_dev, table_hbm, q_hbm, zsend_hbm, k_new_hbm, v_new_hbm, out_hbm, fits_hbm, q_ref, out_ref, recv_k, recv_v, k_new, v_new,
                    new_t, wide, zsend, table_ref, first_vec, second_vec, first_ref, second_ref, named_by_column, fits_vec, *scratch):
    zrecv, send1, recv1, send2 = (scratch[:N_CH], scratch[N_CH:3 * N_CH], scratch[3 * N_CH:5 * N_CH], scratch[5 * N_CH:7 * N_CH])
    zs_sem, zr_sem, s1_sem, r1_sem, s2_sem, r2_sem, in_sem, out_sem = scratch[7 * N_CH:]
    me = lax.axis_index('pool')
    my_z, my_pos = me // PLANE, lax.rem(me, PLANE)
    base = my_z * PLANE
    y, x, c = my_pos // 8, lax.rem(my_pos // 2, RING), lax.rem(my_pos, 2)
    head_dim = q_ref.shape[2]

    def z_peer(d):
        return lax.rem(my_z + d, PLANES) * PLANE + my_pos

    def y_peer(d, dc):
        return base + lax.rem(y + d, RING) * 8 + x * 2 + lax.rem(c + dc, 2)

    def x_peer(d, dc):
        return base + y * 8 + lax.rem(x + d, RING) * 2 + lax.rem(c + dc, 2)

    barrier = pltpu.get_barrier_semaphore()
    peers = [z_peer(d) for d in STEPS] + [peer(d, dc) for d in STEPS for dc in range(2) for peer in (y_peer, x_peer)] + [y_peer(0, 1)]
    for peer in peers:
        pl.semaphore_signal(barrier, inc=1, device_id=(peer,), device_id_type=MESH)

    loads = [pltpu.make_async_copy(src, dst, in_sem.at[i]) for i, (src, dst) in enumerate(
        ((zsend_hbm, zsend), (k_new_hbm, k_new), (v_new_hbm, v_new), (q_hbm, q_ref), (table_hbm, table_ref)))]
    to_smem = [pltpu.make_async_copy(src, dst, in_sem.at[5 + i]) for i, (src, dst) in enumerate(((first_vec, first_ref), (second_vec, second_ref)))]
    fits_copy = pltpu.make_async_copy(fits_vec, fits_hbm, in_sem.at[7])
    for copy in loads:
        copy.start()

    def remote(src, dst, send_sem, recv_sem, peer):
        return pltpu.make_async_remote_copy(
            src_ref=src, dst_ref=dst, send_sem=send_sem, recv_sem=recv_sem, device_id=(peer,), device_id_type=MESH)

    def wait_bytes(ref, sem):
        pltpu.make_async_copy(ref, ref, sem).wait()

    def z_wait(ch, sem):
        wait_bytes(zrecv[ch].at[pl.ds(0, (PLANES - 1) * Z_CAP)], sem.at[ch])

    def wait1(i, sem):
        wait_bytes(recv1[i].at[pl.ds(0, (RING - 1) * GROUP_CAP)], sem.at[i])

    def wait2(i, sem):
        wait_bytes(send2[i].at[pl.ds(0, 2 * RING - 1)], sem.at[i])

    def step1(ch):
        for part in range(2):
            i = 2 * ch + part
            for g in range(RING):
                for s in range(GROUP_CAP):
                    send1[i][g, s] = zrecv[ch][first_ref[part * RING + g, s], part]
            mine = y if part == 0 else x
            recv1[i][pl.ds(mine * GROUP_CAP, GROUP_CAP)] = send1[i][mine]
        for d in STEPS:
            for part in range(2):
                i = 2 * ch + part
                mine, peer = (y, y_peer(d, 0)) if part == 0 else (x, x_peer(d, 0))
                remote(send1[i].at[lax.rem(mine + d, RING)], recv1[i].at[pl.ds(mine * GROUP_CAP, GROUP_CAP)],
                       s1_sem.at[i], r1_sem.at[i], peer).start()

    def step2(ch):
        for part in range(2):
            i = 2 * ch + part
            wait1(i, r1_sem)

            @pl.loop(0, RING)
            def _(to):
                for core in range(2):
                    row = base + ((y * 8 + to * 2) if part == 0 else (to * 8 + x * 2)) + core
                    for src in range(RING):
                        for end in range(PAIR_CAP):
                            send2[i][to * 2 + core, src, end * 16:(end + 1) * 16, :] = recv1[i][second_ref[(part * RING + src) * PAIR_CAP + end, row]]

        recv_k[ch, :, x, c] = send2[2 * ch][x * 2 + c]
        recv_v[ch, y, :, c] = send2[2 * ch + 1][y * 2 + c]
        for d in STEPS + (0,):
            for dc in range(2):
                for part in range(2):
                    if (d, dc) == (0, 0):
                        continue
                    i = 2 * ch + part
                    mine, peer = (x, x_peer(d, dc)) if part == 0 else (y, y_peer(d, dc))
                    dst = recv_k.at[ch, :, x, c] if part == 0 else recv_v.at[ch, y, :, c]
                    remote(send2[i].at[lax.rem(mine + d, RING) * 2 + lax.rem(c + dc, 2)], dst, s2_sem.at[i], r2_sem.at[i], peer).start()

    def out_copy(ch):
        heads = pl.ds(ch * GROUP, GROUP)
        return pltpu.make_async_copy(out_ref.at[:, heads, :], out_hbm.at[:, heads, :], out_sem.at[ch])

    def attend(ch):
        wait2(2 * ch, r2_sem)
        wait2(2 * ch + 1, r2_sem)
        recv = (recv_k, recv_v)
        attend_head(q_ref, lambda part: recv[part][ch].reshape(-1, head_dim), lambda part: new_t[ch, part], out_ref, ch)
        out_copy(ch).start()

    loads[0].wait()
    pl.semaphore_wait(barrier, len(peers))
    for ch in range(N_CH):
        for d in STEPS:
            remote(zsend.at[ch], zrecv[ch].at[pl.ds(my_z * Z_CAP, Z_CAP)], zs_sem.at[ch], zr_sem.at[ch], z_peer(d)).start()
    loads[4].wait()
    table = Table(table_ref[...], per_dev)
    routing(table, my_z, y, x, c, first_vec, second_vec)
    for copy in to_smem:
        copy.start()
    for ch in range(N_CH):
        zrecv[ch][pl.ds(my_z * Z_CAP, Z_CAP)] = zsend[ch]
    for copy in to_smem:
        copy.wait()

    def new_keys():
        for part, block in enumerate((k_new, v_new)):
            loads[1 + part].wait()

            def store(i, h, x):
                new_t[h, part, i * 16:(i + 1) * 16, :] = x
            head_major(lambda i: block[i], wide, store, block.shape[0])
        loads[3].wait()

    for t in range(N_CH + LAG):
        if t < N_CH:
            z_wait(t, zr_sem)
            step1(t)
        if t == 0:
            new_keys()
        if t == 1:
            fits_vec[...] = jnp.broadcast_to(capacity_check(table, named_by_column), fits_vec.shape)
            fits_copy.start()
        if 1 <= t <= N_CH:
            step2(t - 1)
        if t >= LAG:
            attend(t - LAG)
    fits_copy.wait()
    for ch in range(N_CH):
        z_wait(ch, zs_sem)
        out_copy(ch).wait()
    for i in range(2 * N_CH):
        wait1(i, s1_sem)
        wait2(i, s2_sem)


def exchange_attention(table_t, q, zsend, k_new, v_new, per_dev):
    tokens, dim = zsend.shape[3:]
    dtype = q.dtype
    hbm = pl.BlockSpec(memory_space=pl.ANY)
    recv = pltpu.VMEM((N_CH, RING, RING, 2, PAIR_CAP * tokens, dim), dtype)
    tables = [(2 * RING, 128), (2 * RING * PAIR_CAP, table_t.shape[1])]
    return pl.pallas_call(
        functools.partial(exchange_kernel, per_dev),
        out_shape=[jax.ShapeDtypeStruct(q.shape, dtype), jax.ShapeDtypeStruct((8, 128), jnp.int32)],
        in_specs=[hbm] * 5,
        out_specs=[hbm, hbm],
        scratch_shapes=[pltpu.VMEM(q.shape, dtype), pltpu.VMEM(q.shape, dtype), recv, recv,
                        pltpu.VMEM(k_new.shape, dtype), pltpu.VMEM(v_new.shape, dtype), pltpu.VMEM((N_CH, 2, q.shape[0], q.shape[2]), dtype),
                        pltpu.VMEM((4,) + k_new.shape[1:], jnp.float32), pltpu.VMEM(zsend.shape, dtype), pltpu.VMEM(table_t.shape, jnp.int32)]
        + [pltpu.VMEM(shape, jnp.int32) for shape in tables] + [pltpu.SMEM(shape, jnp.int32) for shape in tables]
        + [pltpu.VMEM((PLANE, 128), jnp.float32), pltpu.VMEM((8, 128), jnp.int32)]
        + [pltpu.VMEM((PLANES * Z_CAP, 2, tokens, dim), dtype)] * N_CH
        + [pltpu.VMEM((RING, GROUP_CAP, tokens, dim), dtype)] * (2 * N_CH)
        + [pltpu.VMEM((RING * GROUP_CAP, tokens, dim), dtype)] * (2 * N_CH)
        + [pltpu.VMEM((2 * RING, RING, PAIR_CAP * tokens, dim), dtype)] * (2 * N_CH)
        + [pltpu.SemaphoreType.DMA((N_CH,))] * 2 + [pltpu.SemaphoreType.DMA((2 * N_CH,))] * 4 + [pltpu.SemaphoreType.DMA((N_CH,))] * 2,
        compiler_params=pltpu.CompilerParams(collective_id=0, has_side_effects=True, vmem_limit_bytes=56 << 20),
        name='exchange_attention',
    )(table_t, q, zsend, k_new, v_new)


def attention_kernel(q_ref, kv_ref, new_ref, out_ref):
    head_dim = q_ref.shape[2]
    attend_head(q_ref, lambda part: kv_ref[0, :, part].reshape(-1, head_dim), lambda part: new_ref[0, part], out_ref, 0)


def attention(q, kv, new):
    chunk_len, q_heads, head_dim = q.shape
    return pl.pallas_call(
        attention_kernel,
        grid=(N_CH,),
        out_shape=jax.ShapeDtypeStruct(q.shape, q.dtype),
        in_specs=[pl.BlockSpec((chunk_len, GROUP, head_dim), lambda c: (0, c, 0)),
                  pl.BlockSpec((1,) + kv.shape[1:], lambda c: (c, 0, 0, 0, 0)),
                  pl.BlockSpec((1,) + new.shape[1:], lambda c: (c, 0, 0, 0))],
        out_specs=pl.BlockSpec((chunk_len, GROUP, head_dim), lambda c: (0, c, 0)),
        compiler_params=pltpu.CompilerParams(vmem_limit_bytes=48 << 20),
        name='attention',
    )(q, kv, new)


def by_chunk(k, v):
    n, t, h, d = k.shape
    both = jnp.stack([k, v], axis=1).reshape(n, 2, t, N_CH, h // N_CH, d)
    return both.transpose(0, 3, 1, 4, 2, 5).reshape(n, N_CH, 2 * h // N_CH, t, d)


def solution(mesh):
    n_dev = mesh.shape['pool']

    def padded_exchange(k_pool, v_pool, block_table):
        per_dev = k_pool.shape[0]
        n_pref = block_table.shape[1]
        my_index = lax.axis_index('pool')
        pair_cap = 2
        owners = block_table // per_dev
        owned_here = (owners == my_index).astype(jnp.int32)
        send_slot = jnp.where(owned_here > 0, jnp.cumsum(owned_here, axis=1) - 1, pair_cap)
        dest_dev = jnp.broadcast_to(jnp.arange(n_dev)[:, None], send_slot.shape)
        send_ids = jnp.zeros((n_dev, pair_cap), jnp.int32).at[dest_dev, send_slot].set(block_table % per_dev, mode='drop')
        k_recv = lax.all_to_all(k_pool[send_ids], 'pool', 0, 0, tiled=True)
        v_recv = lax.all_to_all(v_pool[send_ids], 'pool', 0, 0, tiled=True)
        my_owners = lax.dynamic_slice_in_dim(owners, my_index, 1, 0).reshape(-1)
        from_owner = (my_owners[:, None] == jnp.arange(n_dev)[None, :]).astype(jnp.int32)
        slot_rank = jnp.sum(from_owner * (jnp.cumsum(from_owner, axis=0) - 1), axis=1)
        recv_idx = my_owners * pair_cap + slot_rank
        flat = (n_dev * pair_cap,) + k_pool.shape[1:]
        pairs = by_chunk(k_recv.reshape(flat)[recv_idx], v_recv.reshape(flat)[recv_idx])
        parts, t, d = pairs.shape[2:]
        pairs = pairs.reshape(n_pref // PAIR_CAP, PAIR_CAP, N_CH, parts, t, d).transpose(2, 0, 3, 1, 4, 5)
        return pairs.reshape(N_CH, n_pref // PAIR_CAP, parts, PAIR_CAP * t, d)

    def local_step(queries, k_new, v_new, k_pool, v_pool, block_table, write_ids):
        block_len = k_pool.shape[1]
        new_shape = (queries.shape[1] // block_len, block_len) + k_new.shape[2:]
        k_blocks, v_blocks = k_new.reshape(new_shape), v_new.reshape(new_shape)
        k_pool_out, v_pool_out, zsend = prepare(write_ids, block_table.T, k_pool, v_pool, k_blocks, v_blocks)
        fast, fits = exchange_attention(block_table.T, queries[0], zsend, k_blocks, v_blocks, k_pool.shape[0])
        attn_out = lax.cond(
            fits[0, 0] > 0,
            lambda: fast,
            lambda: attention(queries[0], padded_exchange(k_pool, v_pool, block_table), by_chunk(k_new, v_new)[0]))[None]
        return attn_out, k_pool_out, v_pool_out

    row_spec = P('pool')
    return jax.shard_map(local_step, mesh=mesh, in_specs=(row_spec, row_spec, row_spec, row_spec, row_spec, P(), row_spec), out_specs=(row_spec, row_spec, row_spec), check_vma=False)
```

time: 75.9 us -> 72.9 us (0.960)
  Pallas kernels: 71.1 us -> 65.5 us
  local copies, waits for them, and re-layouts: 2.48 us -> 5.77 us
    pallas_call x1, Pallas kernels: 10.3 us -> 4.92 us  [prepare(): pl.pallas_call(prepare_kernel, out_shape=[jax.ShapeDtypeStruct(k_pool.sha...]
    unnamed x3 -> x15, local copies, waits for them, and re-layouts: 1.97 us -> 4.58 us
where the time goes in v1:
time: 72.9 us; the launch traced here: 72.7 us
  Pallas kernels  65.5 us (90%)
  local copies, waits for them, and re-layouts  5.77 us (8%)
  between operations  1.38 us (2%)
    pallas_call x1, Pallas kernels, exchange_attention(): pl.pallas_call(functools.partial(exchange_kernel, per_dev), out_shape=[ja...  60.6 us
    pallas_call x1, Pallas kernels, prepare(): pl.pallas_call(prepare_kernel, out_shape=[jax.ShapeDtypeStruct(k_pool.sha...  4.92 us
    unnamed x15, local copies, waits for them, and re-layouts  4.58 us

profile of v1, /device:TPU:1, one launch (start us, length us, event | category | flops | bytes accessed | tf_op | source)
XLA Modules:
  0.0 72.7 jit_solution(635461620232859600)
XLA Ops:
  0.6 0.0 copy-start.1
  0.6 0.6 copy-done.1
  1.3 0.0 copy-start.2
  1.3 0.0 copy-start.3
  1.3 0.0 copy-start.5
  1.3 0.0 copy-start.6
  1.3 0.0 copy-start.7
  1.3 4.9 %prepare.1 = (bf16[32,16,8,128]{3,2,1,0:T(8,128)(2,1)}, bf16[32,16,8,128]{3,2,1,0:T(8,128)(2,1)}, bf16[8,10,2,16,128]{4,3,2,1,0:T(8,128)(2,1)S(1)}) custom-call(s32[1,8]{1,0:T(1,128)S(1)} %copy-done.1, s32[64,128]{1,0:T(8,128)} %bitcast.60, bf16[32,16,8,128]{3,2,1,0:T(8,128)(2,1)} %k_pool_hbm.1, bf16[32,16,8,128]{3,2,1,0:T(8,128)(2,1)} %v_pool_hbm.1, ...), custom_call_target="tpu_custom_call" | custom-call | tf_op jit(solution)/shard_map/prepare/pallas_call | solution.py:147
  6.2 0.0 copy-start
  6.3 0.8 %copy-done = bf16[8,10,2,16,128]{4,3,2,1,0:T(8,128)(2,1)} copy-done((bf16[8,10,2,16,128]{4,3,2,1,0:T(8,128)(2,1)}, bf16[8,10,2,16,128]{4,3,2,1,0:T(8,128)(2,1)S(1)}, u32[]{:S(2)}) %copy-start) | copy-done | bytes 655384
  7.1 60.6 %exchange_attention.1 = (bf16[128,64,128]{2,1,0:T(8,128)(2,1)}, s32[8,128]{1,0:T(8,128)}) custom-call(s32[64,128]{1,0:T(8,128)} %bitcast.61, bf16[128,64,128]{2,1,0:T(8,128)(2,1)} %bitcast.50, bf16[8,10,2,16,128]{4,3,2,1,0:T(8,128)(2,1)} %copy-done, bf16[8,16,8,128]{3,2,1,0:T(8,128)(2,1)} %bitcast.55, bf16[8,16,8,128]{3,2,1,0:T(8,128)(2,1)} %bitcast.57), custom_call_target="tpu_custom_call" | custom-call | tf_op jit(solution)/shard_map/exchange_attention/pallas_call | solution.py:372
  67.7 1.2 %slice.3 = s32[1,1]{1,0:T(1,128)} slice(s32[8,128]{1,0:T(8,128)} %get-tuple-element.33), slice={[0:1], [0:1]} | slice | bytes 8 | tf_op jit(solution)/shard_map/slice | solution.py:450
  69.5 0.0 copy-done.2
  69.5 0.0 copy-done.3
  69.6 0.0 copy-done.5
  69.6 0.0 copy-done.6
  69.6 0.0 copy-done.7
  69.6 3.1 %copy.30 = bf16[1,128,64,128]{3,2,1,0:T(8,128)(2,1)} copy(bf16[1,128,64,128]{3,2,1,0:T(8,128)(2,1)} %get-tuple-element.64) | data formatting | bytes 4194304
  (1 shorter events, 0.0 us)
Async XLA Ops:
  0.6 0.7 copy-start.1
  1.3 68.3 %copy-start.2 = (bf16[32,16,8,128]{3,2,1,0:T(8,128)(2,1)S(1)}, bf16[32,16,8,128]{3,2,1,0:T(8,128)(2,1)}, u32[]{:S(2)}) copy-start(bf16[32,16,8,128]{3,2,1,0:T(8,128)(2,1)} %k_pool_hbm.1) | copy-start | bytes 3145732
  1.3 68.3 %copy-start.3 = (bf16[32,16,8,128]{3,2,1,0:T(8,128)(2,1)S(1)}, bf16[32,16,8,128]{3,2,1,0:T(8,128)(2,1)}, u32[]{:S(2)}) copy-start(bf16[32,16,8,128]{3,2,1,0:T(8,128)(2,1)} %v_pool_hbm.1) | copy-start | bytes 3145732
  1.3 68.3 %copy-start.5 = (bf16[1,128,8,128]{3,2,1,0:T(8,128)(2,1)S(1)}, bf16[1,128,8,128]{3,2,1,0:T(8,128)(2,1)}, u32[]{:S(2)}) copy-start(bf16[1,128,8,128]{3,2,1,0:T(8,128)(2,1)} %param.10) | copy-start | bytes 786436
  1.3 68.3 %copy-start.6 = (bf16[1,128,8,128]{3,2,1,0:T(8,128)(2,1)S(1)}, bf16[1,128,8,128]{3,2,1,0:T(8,128)(2,1)}, u32[]{:S(2)}) copy-start(bf16[1,128,8,128]{3,2,1,0:T(8,128)(2,1)} %param.11) | copy-start | bytes 786436
  1.3 68.3 %copy-start.7 = (s32[128,64]{0,1:T(8,128)S(1)}, s32[128,64]{0,1:T(8,128)}, u32[]{:S(2)}) copy-start(s32[128,64]{0,1:T(8,128)} %param.14) | copy-start | bytes 98308
  6.2 0.8 %copy-start = (bf16[8,10,2,16,128]{4,3,2,1,0:T(8,128)(2,1)}, bf16[8,10,2,16,128]{4,3,2,1,0:T(8,128)(2,1)S(1)}, u32[]{:S(2)}) copy-start(bf16[8,10,2,16,128]{4,3,2,1,0:T(8,128)(2,1)S(1)} %get-tuple-element.32.zsend_hbm) | copy-start | bytes 1966084

commit v2 on v1

--- a/solution.py
+++ b/solution.py
@@ -219,10 +219,10 @@
                 second_ref[line:line + 1, :] = jnp.clip(found.astype(jnp.int32), 0, GROUP_CAP - 1) + src * GROUP_CAP
 
 
-def exchange_kernel(per_dev, table_hbm, q_hbm, zsend_hbm, k_new_hbm, v_new_hbm, out_hbm, fits_hbm, q_ref, out_ref, recv_k, recv_v, k_new, v_new,
+def exchange_kernel(per_dev, table_hbm, q_hbm, zsend_hbm, k_new_hbm, v_new_hbm, out_ref, fits_hbm, q_ref, recv_k, recv_v, k_new, v_new,
                     new_t, wide, zsend, table_ref, first_vec, second_vec, first_ref, second_ref, named_by_column, fits_vec, *scratch):
     zrecv, send1, recv1, send2 = (scratch[:N_CH], scratch[N_CH:3 * N_CH], scratch[3 * N_CH:5 * N_CH], scratch[5 * N_CH:7 * N_CH])
-    zs_sem, zr_sem, s1_sem, r1_sem, s2_sem, r2_sem, in_sem, out_sem = scratch[7 * N_CH:]
+    zs_sem, zr_sem, s1_sem, r1_sem, s2_sem, r2_sem, in_sem = scratch[7 * N_CH:]
     me = lax.axis_index('pool')
     my_z, my_pos = me // PLANE, lax.rem(me, PLANE)
     base = my_z * PLANE
@@ -306,16 +306,11 @@
                     dst = recv_k.at[ch, :, x, c] if part == 0 else recv_v.at[ch, y, :, c]
                     remote(send2[i].at[lax.rem(mine + d, RING) * 2 + lax.rem(c + dc, 2)], dst, s2_sem.at[i], r2_sem.at[i], peer).start()
 
-    def out_copy(ch):
-        heads = pl.ds(ch * GROUP, GROUP)
-        return pltpu.make_async_copy(out_ref.at[:, heads, :], out_hbm.at[:, heads, :], out_sem.at[ch])
-
     def attend(ch):
         wait2(2 * ch, r2_sem)
         wait2(2 * ch + 1, r2_sem)
         recv = (recv_k, recv_v)
         attend_head(q_ref, lambda part: recv[part][ch].reshape(-1, head_dim), lambda part: new_t[ch, part], out_ref, ch)
-        out_copy(ch).start()
 
     loads[0].wait()
     pl.semaphore_wait(barrier, len(peers))
@@ -347,17 +342,16 @@
             step1(t)
         if t == 0:
             new_keys()
-        if t == 1:
+        if 1 <= t <= N_CH:
+            step2(t - 1)
+        if t == 2:
             fits_vec[...] = jnp.broadcast_to(capacity_check(table, named_by_column), fits_vec.shape)
             fits_copy.start()
-        if 1 <= t <= N_CH:
-            step2(t - 1)
         if t >= LAG:
             attend(t - LAG)
     fits_copy.wait()
     for ch in range(N_CH):
         z_wait(ch, zs_sem)
-        out_copy(ch).wait()
     for i in range(2 * N_CH):
         wait1(i, s1_sem)
         wait2(i, s2_sem)
@@ -371,10 +365,10 @@
     tables = [(2 * RING, 128), (2 * RING * PAIR_CAP, table_t.shape[1])]
     return pl.pallas_call(
         functools.partial(exchange_kernel, per_dev),
-        out_shape=[jax.ShapeDtypeStruct(q.shape, dtype), jax.ShapeDtypeStruct((8, 128), jnp.int32)],
+        out_shape=[pltpu.VMEM(q.shape, dtype), jax.ShapeDtypeStruct((8, 128), jnp.int32)],
         in_specs=[hbm] * 5,
-        out_specs=[hbm, hbm],
-        scratch_shapes=[pltpu.VMEM(q.shape, dtype), pltpu.VMEM(q.shape, dtype), recv, recv,
+        out_specs=[pl.BlockSpec(memory_space=pltpu.VMEM), hbm],
+        scratch_shapes=[pltpu.VMEM(q.shape, dtype), recv, recv,
                         pltpu.VMEM(k_new.shape, dtype), pltpu.VMEM(v_new.shape, dtype), pltpu.VMEM((N_CH, 2, q.shape[0], q.shape[2]), dtype),
                         pltpu.VMEM((4,) + k_new.shape[1:], jnp.float32), pltpu.VMEM(zsend.shape, dtype), pltpu.VMEM(table_t.shape, jnp.int32)]
         + [pltpu.VMEM(shape, jnp.int32) for shape in tables] + [pltpu.SMEM(shape, jnp.int32) for shape in tables]
@@ -383,8 +377,8 @@
         + [pltpu.VMEM((RING, GROUP_CAP, tokens, dim), dtype)] * (2 * N_CH)
         + [pltpu.VMEM((RING * GROUP_CAP, tokens, dim), dtype)] * (2 * N_CH)
         + [pltpu.VMEM((2 * RING, RING, PAIR_CAP * tokens, dim), dtype)] * (2 * N_CH)
-        + [pltpu.SemaphoreType.DMA((N_CH,))] * 2 + [pltpu.SemaphoreType.DMA((2 * N_CH,))] * 4 + [pltpu.SemaphoreType.DMA((N_CH,))] * 2,
-        compiler_params=pltpu.CompilerParams(collective_id=0, has_side_effects=True, vmem_limit_bytes=56 << 20),
+        + [pltpu.SemaphoreType.DMA((N_CH,))] * 2 + [pltpu.SemaphoreType.DMA((2 * N_CH,))] * 4 + [pltpu.SemaphoreType.DMA((N_CH,))],
+        compiler_params=pltpu.CompilerParams(collective_id=0, has_side_effects=True, vmem_limit_bytes=48 << 20),
         name='exchange_attention',
     )(table_t, q, zsend, k_new, v_new)
 

time: 72.9 us -> 66.4 us (0.911)
  local copies, waits for them, and re-layouts: 5.77 us -> 2.49 us
  Pallas kernels: 65.5 us -> 62.5 us
    pallas_call x1, Pallas kernels: 60.6 us -> 57.8 us  [exchange_attention(): pl.pallas_call(functools.partial(exchange_kernel, per_dev), out_shape=[pl...]
    unnamed x15 -> x9, local copies, waits for them, and re-layouts: 4.58 us -> 1.98 us
where the time goes in v2:
time: 66.4 us; the launch traced here: 66.3 us
  Pallas kernels  62.5 us (94%)
  local copies, waits for them, and re-layouts  2.49 us (4%)
  between operations  1.34 us (2%)
    pallas_call x1, Pallas kernels, exchange_attention(): pl.pallas_call(functools.partial(exchange_kernel, per_dev), out_shape=[pl...  57.8 us
    pallas_call x1, Pallas kernels, prepare(): pl.pallas_call(prepare_kernel, out_shape=[jax.ShapeDtypeStruct(k_pool.sha...  4.7 us
    unnamed x9, local copies, waits for them, and re-layouts  1.98 us

profile of v2, /device:TPU:1, one launch (start us, length us, event | category | flops | bytes accessed | tf_op | source)
XLA Modules:
  0.0 66.3 jit_solution(7228348658375938918)
XLA Ops:
  0.6 0.0 copy-start
  0.6 0.6 copy-done
  1.3 0.0 copy-start.1
  1.3 0.0 copy-start.4
  1.3 0.0 copy-start.6
  1.3 4.7 %prepare.1 = (bf16[32,16,8,128]{3,2,1,0:T(8,128)(2,1)}, bf16[32,16,8,128]{3,2,1,0:T(8,128)(2,1)}, bf16[8,10,2,16,128]{4,3,2,1,0:T(8,128)(2,1)S(1)}) custom-call(s32[1,8]{1,0:T(1,128)S(1)} %copy-done, s32[64,128]{1,0:T(8,128)} %bitcast.60, bf16[32,16,8,128]{3,2,1,0:T(8,128)(2,1)} %k_pool_hbm.1, bf16[32,16,8,128]{3,2,1,0:T(8,128)(2,1)} %v_pool_hbm.1, ...), custom_call_target="tpu_custom_call" | custom-call | tf_op jit(solution)/shard_map/prepare/pallas_call | solution.py:147
  6.0 57.8 %exchange_attention.1 = (bf16[128,64,128]{2,1,0:T(8,128)(2,1)S(1)}, s32[8,128]{1,0:T(8,128)S(1)}) custom-call(s32[64,128]{1,0:T(8,128)} %bitcast.61, bf16[128,64,128]{2,1,0:T(8,128)(2,1)} %bitcast.52, bf16[8,10,2,16,128]{4,3,2,1,0:T(8,128)(2,1)S(1)} %get-tuple-element.32.zsend_hbm, bf16[8,16,8,128]{3,2,1,0:T(8,128)(2,1)} %bitcast.57, ...), custom_call_target="tpu_custom_call" | custom-call | tf_op jit(solution)/shard_map/exchange_attention/pallas_call | solution.py:366
  63.8 0.5 slice.3
  64.9 0.0 copy-done.1
  64.9 0.0 copy-done.4
  65.0 0.0 copy-done.6
  65.0 1.3 %copy.30 = bf16[1,128,64,128]{3,2,1,0:T(8,128)(2,1)} copy(bf16[1,128,64,128]{3,2,1,0:T(8,128)(2,1)S(1)} %get-tuple-element.64) | data formatting | bytes 4194304
  (1 shorter events, 0.0 us)
Async XLA Ops:
  0.6 0.7 copy-start
  1.3 63.7 %copy-start.1 = (bf16[32,16,8,128]{3,2,1,0:T(8,128)(2,1)S(1)}, bf16[32,16,8,128]{3,2,1,0:T(8,128)(2,1)}, u32[]{:S(2)}) copy-start(bf16[32,16,8,128]{3,2,1,0:T(8,128)(2,1)} %k_pool_hbm.1) | copy-start | bytes 3145732
  1.3 63.7 %copy-start.4 = (bf16[1,128,8,128]{3,2,1,0:T(8,128)(2,1)S(1)}, bf16[1,128,8,128]{3,2,1,0:T(8,128)(2,1)}, u32[]{:S(2)}) copy-start(bf16[1,128,8,128]{3,2,1,0:T(8,128)(2,1)} %param.10) | copy-start | bytes 786436
  1.3 63.7 %copy-start.6 = (s32[128,64]{0,1:T(8,128)S(1)}, s32[128,64]{0,1:T(8,128)}, u32[]{:S(2)}) copy-start(s32[128,64]{0,1:T(8,128)} %param.14) | copy-start | bytes 98308

commit v3 on v2

--- a/solution.py
+++ b/solution.py
@@ -95,13 +95,15 @@
         return named[:1], rank[:1]
 
 
-def prepare_kernel(wid_ref, table_hbm, k_pool_hbm, v_pool_hbm, k_new_hbm, v_new_hbm, k_out_hbm, v_out_hbm, zsend_ref,
-                   table_ref, k_pool, v_pool, k_new, v_new, idx_vec, idx_smem, wide, in_sem, out_sem, idx_sem):
+def prepare_kernel(wid_hbm, table_hbm, k_pool_hbm, v_pool_hbm, k_new_hbm, v_new_hbm, k_out_hbm, v_out_hbm, zsend_ref,
+                   table_ref, k_pool, v_pool, k_new, v_new, idx_vec, idx_smem, wid_ref, wide, in_sem, out_sem, idx_sem, wid_sem):
     me = lax.axis_index('pool')
     my_z, my_pos = me // PLANE, lax.rem(me, PLANE)
     per_dev = k_pool.shape[0]
     get_table = pltpu.make_async_copy(table_hbm, table_ref, idx_sem)
     get_table.start()
+    get_ids = pltpu.make_async_copy(wid_hbm, wid_ref, wid_sem)
+    get_ids.start()
     loads = [pltpu.make_async_copy(src, dst, in_sem.at[i]) for i, (src, dst) in enumerate(
         ((k_pool_hbm, k_pool), (v_pool_hbm, v_pool), (k_new_hbm, k_new), (v_new_hbm, v_new)))]
     for copy in loads:
@@ -122,6 +124,7 @@
     for copy in pools:
         copy.start()
     to_smem.wait()
+    get_ids.wait()
 
     def send_blocks(part, pool):
         def store(i, h, x):
@@ -143,17 +146,18 @@
 
 def prepare(write_ids, table_t, k_pool, v_pool, k_new, v_new):
     tokens, heads, dim = k_pool.shape[1:]
-    vmem, smem, hbm = (pl.BlockSpec(memory_space=m) for m in (pltpu.VMEM, pltpu.SMEM, pl.ANY))
+    vmem, hbm = (pl.BlockSpec(memory_space=m) for m in (pltpu.VMEM, pl.ANY))
     return pl.pallas_call(
         prepare_kernel,
         out_shape=[jax.ShapeDtypeStruct(k_pool.shape, k_pool.dtype), jax.ShapeDtypeStruct(v_pool.shape, v_pool.dtype),
                    jax.ShapeDtypeStruct((N_CH, Z_CAP, 2, tokens, dim), k_pool.dtype)],
-        in_specs=[smem, hbm, hbm, hbm, hbm, hbm],
+        in_specs=[pl.BlockSpec(memory_space=pltpu.HBM)] + [hbm] * 5,
         out_specs=[hbm, hbm, vmem],
         scratch_shapes=[pltpu.VMEM(table_t.shape, jnp.int32), pltpu.VMEM(k_pool.shape, k_pool.dtype), pltpu.VMEM(k_pool.shape, k_pool.dtype),
                         pltpu.VMEM(k_new.shape, k_pool.dtype), pltpu.VMEM(k_new.shape, k_pool.dtype),
-                        pltpu.VMEM((16, 128), jnp.int32), pltpu.SMEM((16, 128), jnp.int32), pltpu.VMEM((4, tokens, heads, dim), jnp.float32),
-                        pltpu.SemaphoreType.DMA((2 * k_new.shape[0],)), pltpu.SemaphoreType.DMA((2,)), pltpu.SemaphoreType.DMA],
+                        pltpu.VMEM((16, 128), jnp.int32), pltpu.SMEM((16, 128), jnp.int32), pltpu.SMEM(write_ids.shape, jnp.int32),
+                        pltpu.VMEM((4, tokens, heads, dim), jnp.float32),
+                        pltpu.SemaphoreType.DMA((2 * k_new.shape[0],)), pltpu.SemaphoreType.DMA((2,)), pltpu.SemaphoreType.DMA, pltpu.SemaphoreType.DMA],
         compiler_params=pltpu.CompilerParams(vmem_limit_bytes=32 << 20),
         name='prepare',
     )(write_ids, table_t, k_pool, v_pool, k_new, v_new)

time: 66.4 us -> 66 us (level)
  no operation moved by 1% of the time
where the time goes in v3:
time: 66 us; the launch traced here: 65.9 us
  Pallas kernels  62 us (94%)
  local copies, waits for them, and re-layouts  2.49 us (4%)
  between operations  1.34 us (2%)
    pallas_call x1, Pallas kernels, exchange_attention(): pl.pallas_call(functools.partial(exchange_kernel, per_dev), out_shape=[pl...  57.8 us
    pallas_call x1, Pallas kernels, prepare(): pl.pallas_call(prepare_kernel, out_shape=[jax.ShapeDtypeStruct(k_pool.sha...  4.25 us
    unnamed x9, local copies, waits for them, and re-layouts  1.98 us

profile of v3, /device:TPU:1, one launch (start us, length us, event | category | flops | bytes accessed | tf_op | source)
XLA Modules:
  0.0 65.9 jit_solution(12993882565412708981)
XLA Ops:
  0.6 0.0 copy-start
  0.6 0.6 copy-done
  1.3 0.0 copy-start.1
  1.3 0.0 copy-start.4
  1.3 0.0 copy-start.6
  1.3 4.3 %prepare.1 = (bf16[32,16,8,128]{3,2,1,0:T(8,128)(2,1)}, bf16[32,16,8,128]{3,2,1,0:T(8,128)(2,1)}, bf16[8,10,2,16,128]{4,3,2,1,0:T(8,128)(2,1)S(1)}) custom-call(s32[1,8]{1,0:T(1,128)S(1)} %copy-done, s32[64,128]{1,0:T(8,128)} %bitcast.60, bf16[32,16,8,128]{3,2,1,0:T(8,128)(2,1)} %k_pool_hbm.1, bf16[32,16,8,128]{3,2,1,0:T(8,128)(2,1)} %v_pool_hbm.1, ...), custom_call_target="tpu_custom_call" | custom-call | tf_op jit(solution)/shard_map/prepare/pallas_call | solution.py:150
  5.6 57.8 %exchange_attention.1 = (bf16[128,64,128]{2,1,0:T(8,128)(2,1)S(1)}, s32[8,128]{1,0:T(8,128)S(1)}) custom-call(s32[64,128]{1,0:T(8,128)} %bitcast.61, bf16[128,64,128]{2,1,0:T(8,128)(2,1)} %bitcast.52, bf16[8,10,2,16,128]{4,3,2,1,0:T(8,128)(2,1)S(1)} %get-tuple-element.32.zsend_hbm, bf16[8,16,8,128]{3,2,1,0:T(8,128)(2,1)} %bitcast.57, ...), custom_call_target="tpu_custom_call" | custom-call | tf_op jit(solution)/shard_map/exchange_attention/pallas_call | solution.py:370
  63.3 0.5 slice.3
  64.5 0.0 copy-done.1
  64.5 0.0 copy-done.4
  64.5 0.0 copy-done.6
  64.5 1.3 %copy.30 = bf16[1,128,64,128]{3,2,1,0:T(8,128)(2,1)} copy(bf16[1,128,64,128]{3,2,1,0:T(8,128)(2,1)S(1)} %get-tuple-element.64) | data formatting | bytes 4194304
  (1 shorter events, 0.0 us)
Async XLA Ops:
  0.6 0.7 copy-start
  1.3 63.2 %copy-start.1 = (bf16[32,16,8,128]{3,2,1,0:T(8,128)(2,1)S(1)}, bf16[32,16,8,128]{3,2,1,0:T(8,128)(2,1)}, u32[]{:S(2)}) copy-start(bf16[32,16,8,128]{3,2,1,0:T(8,128)(2,1)} %k_pool_hbm.1) | copy-start | bytes 3145732
  1.3 63.2 %copy-start.4 = (bf16[1,128,8,128]{3,2,1,0:T(8,128)(2,1)S(1)}, bf16[1,128,8,128]{3,2,1,0:T(8,128)(2,1)}, u32[]{:S(2)}) copy-start(bf16[1,128,8,128]{3,2,1,0:T(8,128)(2,1)} %param.10) | copy-start | bytes 786436
  1.3 63.2 %copy-start.6 = (s32[128,64]{0,1:T(8,128)S(1)}, s32[128,64]{0,1:T(8,128)}, u32[]{:S(2)}) copy-start(s32[128,64]{0,1:T(8,128)} %param.14) | copy-start | bytes 98308
